TPU v7x, 32 devices: a whole 2x2x4 slice. The times are simulated.
32 devices in a mesh: wide: 16 (over z, y, x), narrow: 2 (over core).
Axes of the slice: x: 2, y: 2, z: 4, core: 2. Of those that a mesh axis runs over, the one named last changes fastest.
Arguments:
- tokens: bfloat16 [2048, 2048], P('wide'), may hold values from -6 to 6
- expert_ids: int32 [2048, 6], P('wide'), may hold values from 0 to 15, all different within a row; in each aligned block of 128 rows (0 to 127, 128 to 255, ...) at most 64 rows name the same one
- gate_weights: float32 [2048, 6], P('wide'), may hold values from 0.05 to 0.6
- shared_gate: bfloat16 [2048, 2816], P('wide', 'narrow'), may hold values from -0.125 to 0.125
- shared_up: bfloat16 [2048, 2816], P('wide', 'narrow'), may hold values from -0.125 to 0.125
- shared_down: bfloat16 [2816, 2048], P('narrow', 'wide'), may hold values from -0.109375 to 0.109375
- expert_gate: bfloat16 [16, 2048, 1408], P('wide', None, 'narrow'), may hold values from -0.125 to 0.125
- expert_up: bfloat16 [16, 2048, 1408], P('wide', None, 'narrow'), may hold values from -0.125 to 0.125
- expert_down: bfloat16 [16, 1408, 2048], P('wide', 'narrow'), may hold values from -0.15625 to 0.15625
Outputs:
- moe_out: bfloat16 [2048, 2048], P('wide', 'narrow')
Inputs may be any that keep to these rules, and one draw needn't show every extreme that they name: `expert_ids`: the 6 ids of a row differ. Among the 128 rows of one index of wide, no expert is named by more than 64 rows.
All inputs are finite; a program needn't handle non-finite values.
Results may differ from a plain program's by a relative error of at most 0.0075.
Values may be sent and summed in bfloat16 or wider, within the bound.
A program may use at most 128 MiB of HBM per device.

v0:
```python
import jax
import jax.numpy as jnp
from jax import lax
from jax.sharding import PartitionSpec as P


def expert_ffn(received, w_gate, w_up, w_down):
    senders, items, width = received.shape
    flat_rows = received.reshape(senders * items, width)
    gate_part = jnp.dot(flat_rows, w_gate, preferred_element_type=jnp.float32)
    up_part = jnp.dot(flat_rows, w_up, preferred_element_type=jnp.float32)
    hidden = (jax.nn.silu(gate_part) * up_part).astype(jnp.bfloat16)
    partial_value = jnp.dot(hidden, w_down, preferred_element_type=jnp.float32).astype(jnp.bfloat16)
    return partial_value.reshape(senders, items, w_down.shape[1])


def body(
    tokens,
    expert_ids,
    gate_weights,
    shared_gate,
    shared_up,
    shared_down,
    expert_gate,
    expert_up,
    expert_down,
):
    tok_count, width = tokens.shape
    top_count = expert_ids.shape[1]
    experts = lax.axis_size("wide") * expert_gate.shape[0]
    capacity = min(tok_count, 4 * tok_count * top_count // (3 * experts))
    narrow_count = lax.axis_size("narrow")
    w_gate = expert_gate[0]
    w_up = expert_up[0]
    w_down = expert_down[0]
    pairs = tok_count * top_count
    flat_ids = expert_ids.reshape(pairs)
    onehot = (flat_ids[:, None] == jnp.arange(experts, dtype=jnp.int32)[None, :]).astype(jnp.int32)
    before = jnp.cumsum(onehot, axis=0) - onehot
    slot_pos = jnp.sum(before * onehot, axis=1)
    target_slot = flat_ids * capacity + slot_pos
    source = (
        jnp.full((experts * capacity,), -1, jnp.int32)
        .at[target_slot]
        .set(jnp.arange(pairs, dtype=jnp.int32))
    )
    filled = source >= 0
    token_of = jnp.where(filled, source // top_count, 0)
    outgoing = jnp.where(filled[:, None], tokens[token_of], jnp.zeros((), jnp.bfloat16))
    outgoing = outgoing.reshape(experts, capacity, width)
    quarter = capacity // narrow_count
    own_rows = lax.dynamic_slice_in_dim(outgoing, lax.axis_index("narrow") * quarter, quarter, 1)
    arrived = lax.all_to_all(own_rows, "wide", split_axis=0, concat_axis=0, tiled=True)
    joined = lax.all_gather(arrived, "narrow", axis=1, tiled=True)
    partial_value = expert_ffn(joined, w_gate, w_up, w_down)
    expert_out = (
        lax.psum_scatter(partial_value, "narrow", scatter_dimension=2, tiled=True)
        .astype(jnp.float32)
        .astype(jnp.bfloat16)
    )
    returned = lax.all_to_all(expert_out, "wide", split_axis=0, concat_axis=0, tiled=True)
    returned_rows = returned.reshape(experts * capacity, returned.shape[2])
    pair_rows = returned_rows[target_slot].astype(jnp.float32)
    weighted = gate_weights.reshape(pairs, 1) * pair_rows
    routed = jnp.sum(weighted.reshape(tok_count, top_count, returned.shape[2]), axis=1)
    gate_sum = jnp.dot(
        tokens,
        lax.all_gather(shared_gate, "wide", axis=0, tiled=True),
        preferred_element_type=jnp.float32,
    )
    up_sum = jnp.dot(
        tokens,
        lax.all_gather(shared_up, "wide", axis=0, tiled=True),
        preferred_element_type=jnp.float32,
    )
    shared_hidden = (jax.nn.silu(gate_sum) * up_sum).astype(jnp.bfloat16)
    shared_terms = jnp.dot(
        shared_hidden,
        lax.all_gather(shared_down, "wide", axis=1, tiled=True),
        preferred_element_type=jnp.float32,
    )
    shared = lax.psum_scatter(shared_terms, "narrow", scatter_dimension=1, tiled=True)
    return (shared + routed).astype(jnp.bfloat16)


def solution(mesh):
    in_specs = (
        P("wide", None),
        P("wide", None),
        P("wide", None),
        P("wide", "narrow"),
        P("wide", "narrow"),
        P("narrow", "wide"),
        P("wide", None, "narrow"),
        P("wide", None, "narrow"),
        P("wide", "narrow", None),
    )
    out_specs = P("wide", "narrow")
    return jax.shard_map(body, mesh=mesh, in_specs=in_specs, out_specs=out_specs, check_vma=False)
```

profile of v0, /device:TPU:17, one launch (start us, length us, event | category | flops | bytes accessed | tf_op | source)
XLA Modules:
  0.0 459.3 jit_solution(8130816217768334769)
XLA Ops:
  7.4 0.0 copy-start
  7.4 0.0 copy-start.1
  7.4 0.0 all-gather.11.cloned.1.call-start
  7.4 0.8 broadcast_multiply_fusion
  8.2 0.9 copy.13
  9.1 0.1 eq.29
  9.3 0.1 eq.25
  9.4 0.1 copy.12
  9.5 0.1 mul.50
  9.7 1.7 reduce-window.6
  11.4 0.3 slice_reduce_fusion
  11.7 0.1 fusion.14
  11.8 3.4 scatter_custom_fusion
  15.2 0.1 broadcast_in_dim.27
  15.3 0.1 constant_dynamic-slice_fusion
  15.4 0.0 copy-done.1
  15.4 6.0 %gather_fusion = bf16[1024,2048]{1,0:T(8,128)(2,1)} fusion(bf16[128,2048]{1,0:T(8,128)(2,1)S(1)} %copy-done.1, s32[1024]{0:T(1024)S(1)} %fusion.17), kind=kCustom, calls=%fused_computation | custom fusion | bytes 8392704 | tf_op jit(solution)/shard_map/gather | solution.py:49
  21.4 2.0 dynamic-slice_select_fusion
  23.4 53.3 %all_to_all.10 = bf16[16,32,2048]{2,1,0:T(8,128)(2,1)} all-to-all(bf16[16,32,2048]{2,1,0:T(8,128)(2,1)S(1)} %dynamic-slice_select_fusion), channel_id=1, replica_groups=mesh['wide'=16,'narrow'=2] {'wide'}, dimensions={0} | all-to-all | bytes 4194304 | tf_op jit(solution)/shard_map/all_to_all | solution.py:53
  76.7 0.0 all-gather.11.cloned.1.call-update
  76.7 0.0 reduce-scatter.5.cloned.1.call-start
  76.8 14.9 %all-gather.11.cloned.1.call-done = bf16[16,64,2048]{2,1,0:T(8,128)(2,1)} async-done(((bf16[16,32,2048]{2,1,0:T(8,128)(2,1)}), bf16[16,64,2048]{2,1,0:T(8,128)(2,1)}) %all-gather.11.cloned.1.call-update) | async-done | bytes 4194320 | tf_op jit(solution)/shard_map/all_gather | solution.py:54
  91.7 7.9 %fusion.1 = f32[1024,704]{0,1:T(8,128)} fusion(bf16[1024,2048]{1,0:T(8,128)(2,1)} %bitcast.48, bf16[1,2048,704]{1,2,0:T(8,128)(2,1)} %param.16), kind=kOutput, calls=%fused_computation.6 | convolution fusion | flops 2952790016 | bytes 9961472 | tf_op jit(solution)/shard_map/dot_general | solution.py:11
  99.6 0.0 copy-done
  99.6 11.3 %convolution_convert_fusion = bf16[1024,2048]{1,0:T(8,128)(2,1)} fusion(bf16[1,704,2048]{2,1,0:T(8,128)(2,1)S(1)} %copy-done, f32[1024,704]{0,1:T(8,128)} %fusion.1, bf16[1024,2048]{1,0:T(8,128)(2,1)} %bitcast.49, bf16[1,2048,704]{1,2,0:T(8,128)(2,1)} %param.15), kind=kOutput, calls=%fused_computation.4 | convolution fusion | flops 5912002560 | bytes 17039360 | tf_op jit(solution)/shard_map/dot_general | solution.py:13
  110.9 0.0 reduce-scatter.5.cloned.1.call-update
  110.9 0.0 all-gather.5.cloned.1.call-start
  110.9 0.5 all-gather.5.cloned.1.call-update
  111.5 0.0 all-gather.7.cloned.1.call-start
  111.5 0.5 all-gather.7.cloned.1.call-update
  112.0 0.0 all-gather.9.cloned.1.call-start
  112.1 0.5 all-gather.9.cloned.1.call-update
  112.6 11.4 %reduce-scatter.5.cloned.1.call-done = bf16[16,64,1024]{2,1,0:T(8,128)(2,1)} async-done(((bf16[16,64,2048]{2,1,0:T(8,128)(2,1)}), bf16[16,64,1024]{2,1,0:T(8,128)(2,1)}) %reduce-scatter.5.cloned.1.call-update) | async-done | bytes 2097168 | tf_op jit(solution)/shard_map/reduce_scatter | solution.py:57
  124.1 6.4 %all-to-all-start.1 = ((bf16[16,64,1024]{2,1,0:T(8,128)(2,1)}), bf16[16,64,1024]{2,1,0:T(8,128)(2,1)}, u32[]{:S(2)}, u32[]{:S(2)}) async-start(bf16[16,64,1024]{2,1,0:T(8,128)(2,1)} %reduce-scatter.5.cloned.1.call-done), calls=%async_computation.3 | async-start | bytes 4194304 | tf_op jit(solution)/shard_map/all_to_all | solution.py:61
  130.5 0.2 reduce-scatter.3.cloned.1.call-start
  130.7 98.5 %all-gather.5.cloned.1.call-done = bf16[2048,1408]{1,0:T(8,128)(2,1)} async-done(((bf16[128,1408]{1,0:T(8,128)(2,1)}), bf16[2048,1408]{1,0:T(8,128)(2,1)}) %all-gather.5.cloned.1.call-update) | async-done | bytes 5767184 | tf_op jit(solution)/shard_map/all_gather | solution.py:68
  229.2 4.5 fusion.24
  233.7 0.0 copy-start.2
  233.7 85.6 %all-gather.7.cloned.1.call-done = bf16[2048,1408]{1,0:T(8,128)(2,1)} async-done(((bf16[128,1408]{1,0:T(8,128)(2,1)}), bf16[2048,1408]{1,0:T(8,128)(2,1)}) %all-gather.7.cloned.1.call-update) | async-done | bytes 5767184 | tf_op jit(solution)/shard_map/all_gather | solution.py:73
  319.3 109.3 %all-gather.9.cloned.1.call-done = bf16[1408,2048]{1,0:T(8,128)(2,1)} async-done(((bf16[1408,128]{1,0:T(8,128)(2,1)}), bf16[1408,2048]{1,0:T(8,128)(2,1)}) %all-gather.9.cloned.1.call-update) | async-done | bytes 5767184 | tf_op jit(solution)/shard_map/all_gather | solution.py:79
  428.5 7.5 %fusion.10 = f32[128,2048]{1,0:T(8,128)} fusion(bf16[1408,2048]{1,0:T(8,128)(2,1)} %all-gather.9.cloned.1.call-done, bf16[128,2048]{1,0:T(8,128)(2,1)S(1)} %copy-done.1, bf16[2048,1408]{1,0:T(8,128)(2,1)} %all-gather.7.cloned.1.call-done, f32[128,1408]{1,0:T(8,128)} %fusion.24), kind=kOutput, calls=%fused_computation.14 | convolution fusion | flops 1477476352 | bytes 13828096 | tf_op jit(solution)/shard_map/dot_general | solution.py:77
  436.0 0.0 reduce-scatter.3.cloned.1.call-update
  436.0 0.0 copy-done.2
  436.0 0.1 copy.11
  436.1 0.0 all-to-all-done.1
  436.2 6.4 %gather_fusion.1 = bf16[768,1024]{1,0:T(8,128)(2,1)} fusion(bf16[1024,1024]{1,0:T(8,128)(2,1)} %bitcast.7, s32[1024]{0:T(1024)S(1)} %pad_clamp_fusion), kind=kCustom, calls=%fused_computation.1 | custom fusion | bytes 3148800 | tf_op jit(solution)/shard_map/gather | solution.py:63
  442.6 4.0 reshape.78
  446.5 3.6 multiply_reduce_fusion
  450.1 0.0 reduce-scatter.3.cloned.1.call-done
  450.1 1.8 add_convert_fusion
  (7 shorter events, 0.1 us)
Async XLA Ops:
  7.4 92.2 %copy-start = (bf16[1,704,2048]{2,1,0:T(8,128)(2,1)S(1)}, bf16[1,704,2048]{2,1,0:T(8,128)(2,1)}, u32[]{:S(2)}) copy-start(bf16[1,704,2048]{2,1,0:T(8,128)(2,1)} %param.17) | copy-start | bytes 8650756
  7.4 8.0 %copy-start.1 = (bf16[128,2048]{1,0:T(8,128)(2,1)S(1)}, bf16[128,2048]{1,0:T(8,128)(2,1)}, u32[]{:S(2)}) copy-start(bf16[128,2048]{1,0:T(8,128)(2,1)} %param.9) | copy-start | bytes 1572868
  7.4 84.3 %all-gather.11.cloned.1.call-start = ((), (), s32[]{:S(2)}) async-start(), calls=%async_computation.8 | async-start | bytes 6291456 | tf_op jit(solution)/shard_map/all_gather | solution.py:54
  76.7 47.3 %reduce-scatter.5.cloned.1.call-start = ((), (), s32[]{:S(2)}) async-start(), calls=%async_computation.9 | async-start | bytes 6291456 | tf_op jit(solution)/shard_map/reduce_scatter | solution.py:57
  110.9 118.3 %all-gather.5.cloned.1.call-start = ((), (), s32[]{:S(2)}) async-start(), calls=%async_computation.4 | async-start | bytes 6127616 | tf_op jit(solution)/shard_map/all_gather | solution.py:68
  111.5 207.8 %all-gather.7.cloned.1.call-start = ((), (), s32[]{:S(2)}) async-start(), calls=%async_computation.5 | async-start | bytes 6127616 | tf_op jit(solution)/shard_map/all_gather | solution.py:73
  112.0 316.5 %all-gather.9.cloned.1.call-start = ((), (), s32[]{:S(2)}) async-start(), calls=%async_computation.6 | async-start | bytes 6127616 | tf_op jit(solution)/shard_map/all_gather | solution.py:79
  124.1 312.1 %all-to-all-start.1 = ((bf16[16,64,1024]{2,1,0:T(8,128)(2,1)}), bf16[16,64,1024]{2,1,0:T(8,128)(2,1)}, u32[]{:S(2)}, u32[]{:S(2)}) async-start(bf16[16,64,1024]{2,1,0:T(8,128)(2,1)} %reduce-scatter.5.cloned.1.call-done), calls=%async_computation.3 | async-start | bytes 4194304 | tf_op jit(solution)/shard_map/all_to_all | solution.py:61
  130.5 319.7 %reduce-scatter.3.cloned.1.call-start = ((), (), s32[]{:S(2)}) async-start(), calls=%async_computation.7 | async-start | bytes 1572864 | tf_op jit(solution)/shard_map/reduce_scatter | solution.py:82
  233.7 202.3 %copy-start.2 = (f32[128,6]{0,1:T(8,128)S(1)}, f32[128,6]{0,1:T(8,128)}, u32[]{:S(2)}) copy-start(f32[128,6]{0,1:T(8,128)} %param.11) | copy-start | bytes 9220
Sparse Core Ops, SparseCore 0:
  76.8 14.8 all-gather.10
  111.0 13.0 reduce-scatter.4
  436.1 8.9 reduce-scatter.2
Sparse Core Ops, SparseCore 1:
  114.1 115.1 all-gather.4
  231.8 87.4 all-gather.6
  321.9 106.6 all-gather.8
where the time goes:
time: 463 us; the launch traced here: 459 us
  waiting for transfers between devices  321 us (69%)
  blocking collectives  53.3 us (12%)
  matrix products  31.1 us (7%)
  local copies, waits for them, and re-layouts  21.7 us (5%)
  between operations  14.9 us (3%)
  other arithmetic  10.1 us (2%)
  starting transfers between devices  6.8 us (1%)
    all_gather x1, waiting for transfers between devices, body(): lax.all_gather(shared_down, 'wide', axis=1, tiled=True)  109 us
    all_gather x1, waiting for transfers between devices, body(): lax.all_gather(shared_gate, 'wide', axis=0, tiled=True)  98.5 us
    all_gather x1, waiting for transfers between devices, body(): lax.all_gather(shared_up, 'wide', axis=0, tiled=True)  85.6 us
    all_to_all x1, blocking collectives, body(): lax.all_to_all(own_rows, 'wide', split_axis=0, concat_axis=0, tiled=True)  53.3 us
    all_gather x1, waiting for transfers between devices, body(): joined = lax.all_gather(arrived, 'narrow', axis=1, tiled=True)  14.9 us
    reduce_scatter x1, waiting for transfers between devices, body(): lax.psum_scatter(partial_value, 'narrow', scatter_dimension=2, tiled=True)  11.4 us
    dot_general x1, matrix products, expert_ffn(): jnp.dot(hidden, w_down, preferred_element_type=jnp.float32)  11.3 us
  transfers between devices with their start and end apart: 7, of which 5 were waited for; matrix products, arithmetic and copies ran while one was open for 6% of the time, Pallas kernels for 0%

commit v1 on v0

--- a/solution.py
+++ b/solution.py
@@ -1,6 +1,10 @@
+import functools
+
 import jax
 import jax.numpy as jnp
 from jax import lax
+from jax.experimental import pallas as pl
+from jax.experimental.pallas import tpu as pltpu
 from jax.sharding import PartitionSpec as P
 
 
@@ -14,7 +18,7 @@
     return partial_value.reshape(senders, items, w_down.shape[1])
 
 
-def body(
+def dispatch_body(
     tokens,
     expert_ids,
     gate_weights,
@@ -83,6 +87,445 @@
     return (shared + routed).astype(jnp.bfloat16)
 
 
+MESH = pl.DeviceIdType.MESH
+ANY = pl.BlockSpec(memory_space=pl.ANY)
+VMEM = pl.BlockSpec(memory_space=pltpu.VMEM)
+LANES = 128
+PLANE = 4
+
+
+def plan(tok_count, top_count, experts, wide_count):
+    capacity = min(tok_count, 4 * tok_count * top_count // (3 * experts))
+    return capacity, wide_count * tok_count <= 4 * experts * capacity
+
+
+def greet(devices):
+    barrier = pltpu.get_barrier_semaphore()
+    for device in devices:
+        pl.semaphore_signal(barrier, inc=1, device_id=device, device_id_type=MESH)
+    pl.semaphore_wait(barrier, len(devices))
+
+
+def gather_kernel(
+    wide, tok, gate, up, down, dense, every, all_gate, all_up, all_down, weight, send, recv, local
+):
+    me = lax.axis_index("wide")
+    core = lax.axis_index("narrow")
+    lines = wide // PLANE
+    count = tok.shape[0]
+    rows = count // 2
+    half = rows // 2
+    pieces = gate.shape[1] // LANES
+    greet([(me ^ k, core) for k in range(1, wide)] + [(me, 1 - core)])
+
+    def region(chip, side=None):
+        start = chip * count + core * rows
+        if side is None:
+            return every.at[pl.ds(pl.multiple_of(start, rows), rows)]
+        return every.at[pl.ds(pl.multiple_of(start + side * half, half), half)]
+
+    def copy(number, source, target, device):
+        return pltpu.make_async_remote_copy(
+            src_ref=source,
+            dst_ref=target,
+            send_sem=send.at[number],
+            recv_sem=recv.at[number],
+            device_id=device,
+            device_id_type=MESH,
+        )
+
+    x_peer, y_peer, twin = (me ^ 1, core), (me ^ 2, core), (me, 1 - core)
+    Z, X, Y = 0, lines, 2 * lines
+    XD, YD, T = 3 * lines, 4 * lines, 5 * lines
+    W = T + 5 * lines
+    started = []
+
+    def start(item):
+        item.start()
+        started.append(item)
+
+    def arrive(number, place):
+        copy(number, place, place, twin).wait_recv()
+        start(copy(T + number, place, place, twin))
+
+    own = pltpu.make_async_copy(
+        tok, every.at[pl.ds(pl.multiple_of(me * count, count), count)], local.at[0]
+    )
+    own.start()
+    mine = tok.at[pl.ds(pl.multiple_of(core * rows, rows), rows)]
+    start(copy(X, mine, region(me), x_peer))
+    start(copy(Y, mine, region(me), y_peer))
+    for d in range(1, lines):
+        start(copy(Z + d, mine, region(me), (me ^ (PLANE * d), core)))
+    dense_copies = []
+    for k in range(1, wide):
+        item = copy(W + k, dense.at[me ^ k], weight.at[me], (me ^ k, core))
+        item.start()
+        dense_copies.append(item)
+    dense_own = pltpu.make_async_copy(dense.at[me], weight.at[me], local.at[1])
+    dense_own.start()
+
+    def line(d):
+        chip = me ^ (PLANE * d)
+        arrive(Z + d, region(chip))
+        start(copy(X + d, region(chip), region(chip), x_peer))
+        start(copy(Y + d, region(chip), region(chip), y_peer))
+
+    def beside(d):
+        chip = me ^ 1 ^ (PLANE * d)
+        arrive(X + d, region(chip))
+        start(copy(YD + d, region(chip, 1), region(chip, 1), y_peer))
+        chip = me ^ 2 ^ (PLANE * d)
+        arrive(Y + d, region(chip))
+        start(copy(XD + d, region(chip, 0), region(chip, 0), x_peer))
+
+    def shared_copies(k):
+        to = me ^ k
+        part = pl.ds(pl.multiple_of(to * LANES, LANES), LANES)
+        place = pl.ds(pl.multiple_of(me * LANES, LANES), LANES)
+        base = W + k
+        return [
+            copy(base + wide, gate.at[:, part], all_gate.at[place], (to, core)),
+            copy(base + 2 * wide, up.at[:, part], all_up.at[place], (to, core)),
+            copy(base + 3 * wide, down.at[part], all_down.at[:, place], (to, core)),
+        ]
+
+    beside(0)
+    for d in range(1, lines):
+        line(d)
+        if d >= 2:
+            beside(d - 1)
+
+    for k in range(1, wide):
+
+        @pl.when((me ^ k) < pieces)
+        def _():
+            for item in shared_copies(k):
+                item.start()
+
+    @pl.when(me < pieces)
+    def _():
+        part = pl.ds(pl.multiple_of(me * LANES, LANES), LANES)
+        items = [
+            pltpu.make_async_copy(gate.at[:, part], all_gate.at[part], local.at[2]),
+            pltpu.make_async_copy(up.at[:, part], all_up.at[part], local.at[3]),
+            pltpu.make_async_copy(down.at[part], all_down.at[:, part], local.at[4]),
+        ]
+        for item in items:
+            item.start()
+        for item in items:
+            item.wait()
+
+    @pl.when(me >= pieces)
+    def _():
+        all_gate[...] = jnp.zeros_like(all_gate)
+        all_up[...] = jnp.zeros_like(all_up)
+        all_down[...] = jnp.zeros_like(all_down)
+
+    beside(lines - 1)
+    for d in range(lines):
+        arrive(XD + d, region(me ^ 3 ^ (PLANE * d), 0))
+        arrive(YD + d, region(me ^ 3 ^ (PLANE * d), 1))
+    own.wait()
+    dense_own.wait()
+    for item in dense_copies:
+        item.wait()
+    for k in range(1, wide):
+
+        @pl.when((me ^ k) < pieces)
+        def _():
+            for item in shared_copies(k):
+                item.wait_send()
+
+        @pl.when(me < pieces)
+        def _():
+            place = pl.ds(pl.multiple_of((me ^ k) * LANES, LANES), LANES)
+            landed = (all_gate.at[place], all_up.at[place], all_down.at[:, place])
+            for number, target in enumerate(landed):
+                copy(W + k + (number + 1) * wide, target, target, twin).wait_recv()
+
+    for item in started:
+        item.wait_send()
+
+    def other(chip, side=None):
+        start = chip * count + (1 - core) * rows
+        if side is None:
+            return every.at[pl.ds(pl.multiple_of(start, rows), rows)]
+        return every.at[pl.ds(pl.multiple_of(start + side * half, half), half)]
+
+    for d in range(lines):
+        if d > 0:
+            place = other(me ^ (PLANE * d))
+            copy(T + Z + d, place, place, twin).wait_recv()
+        for base, flip, side in ((X, 1, None), (Y, 2, None), (XD, 3, 0), (YD, 3, 1)):
+            place = other(me ^ flip ^ (PLANE * d), side)
+            copy(T + base + d, place, place, twin).wait_recv()
+
+
+def gather(wide, tokens, gate, up, down, dense):
+    count, width = tokens.shape
+    lines = wide // PLANE
+    sems = 10 * lines + 4 * wide
+    bf16 = jnp.bfloat16
+    return pl.pallas_call(
+        functools.partial(gather_kernel, wide),
+        out_shape=(
+            jax.ShapeDtypeStruct((wide * count, width), bf16),
+            jax.ShapeDtypeStruct((wide * gate.shape[0], LANES), bf16),
+            jax.ShapeDtypeStruct((wide * gate.shape[0], LANES), bf16),
+            jax.ShapeDtypeStruct((LANES, wide * down.shape[1]), bf16),
+            jax.ShapeDtypeStruct((wide, 8, count), jnp.float32),
+        ),
+        in_specs=[VMEM] * 5,
+        out_specs=[VMEM] * 5,
+        scratch_shapes=[
+            pltpu.SemaphoreType.DMA((sems,)),
+            pltpu.SemaphoreType.DMA((sems,)),
+            pltpu.SemaphoreType.DMA((5,)),
+        ],
+        compiler_params=pltpu.CompilerParams(
+            collective_id=0, has_side_effects=True, vmem_limit_bytes=60 << 20
+        ),
+    )(tokens, gate, up, down, dense)
+
+
+def expert_kernel(group, slots, x, w, w_gate, w_up, w_down, s_gate, s_up, s_down, own, rows, slot_w, both):
+    count = w.shape[2]
+    f32, bf16 = jnp.float32, jnp.bfloat16
+    hidden_count = w_gate.shape[1]
+    lane_r = lax.broadcasted_iota(jnp.int32, (count, count), 0)
+    lane_c = lax.broadcasted_iota(jnp.int32, (count, count), 1)
+    upper = (lane_r <= lane_c).astype(f32).astype(bf16)
+    slot = lax.broadcasted_iota(jnp.int32, (slots, count), 0).astype(f32)
+    picks = []
+    for b in range(group):
+        weight = w[b]
+        chosen = (weight > 0.0).astype(f32)
+        rank = jnp.dot(chosen.astype(bf16), upper, preferred_element_type=f32)
+        where = jnp.where(chosen > 0.0, rank - 1.0, -1.0)[0:1]
+        pick = (jnp.broadcast_to(where, (slots, count)) == slot).astype(f32)
+        picks.append(pick)
+        place = pl.ds(b * slots, slots)
+        slot_w[place] = jnp.sum(pick * weight[0:1], axis=1, keepdims=True)
+        block = x[pl.ds(b * count, count)]
+        rows[place] = jnp.dot(pick.astype(bf16), block, preferred_element_type=f32).astype(bf16)
+    gate = jnp.dot(rows[...], w_gate[...], preferred_element_type=f32)
+    up = jnp.dot(rows[...], w_up[...], preferred_element_type=f32)
+    hidden = (jax.nn.silu(gate) * up * slot_w[...]).astype(bf16)
+    for b in range(group):
+        spread = jnp.dot(
+            picks[b].T.astype(bf16),
+            hidden[b * slots : (b + 1) * slots],
+            preferred_element_type=f32,
+        )
+        both[pl.ds(b * count, count), :hidden_count] = spread.astype(bf16)
+    gate = jnp.dot(x[...], s_gate[...], preferred_element_type=f32)
+    up = jnp.dot(x[...], s_up[...], preferred_element_type=f32)
+    shared = (jax.nn.silu(gate) * up).astype(bf16)
+    width = own.shape[3]
+    routed = both[...]
+    for h in range(own.shape[0]):
+        columns = slice(h * width, (h + 1) * width)
+        part = jnp.dot(routed, w_down[:, columns], preferred_element_type=f32)
+        part += jnp.dot(shared, s_down[:, columns], preferred_element_type=f32)
+        own[h] = part.astype(bf16).reshape(group, count, width)
+
+
+def expert(slots, every, weight, w_gate, w_up, w_down, s_gate, s_up, s_down, narrow):
+    wide, _, count = weight.shape
+    width = every.shape[1]
+    group = 4
+    whole = lambda a: pl.BlockSpec(a.shape, lambda i: (0, 0))
+    return pl.pallas_call(
+        functools.partial(expert_kernel, group, slots),
+        grid=(wide // group,),
+        out_shape=jax.ShapeDtypeStruct((narrow, wide, count, width // narrow), jnp.bfloat16),
+        in_specs=[
+            pl.BlockSpec((group * count, width), lambda i: (i, 0)),
+            pl.BlockSpec((group, 8, count), lambda i: (i, 0, 0)),
+            whole(w_gate),
+            whole(w_up),
+            whole(w_down),
+            whole(s_gate),
+            whole(s_up),
+            whole(s_down),
+        ],
+        out_specs=pl.BlockSpec((narrow, group, count, width // narrow), lambda i: (0, i, 0, 0)),
+        scratch_shapes=[
+            pltpu.VMEM((group * slots, width), jnp.bfloat16),
+            pltpu.VMEM((group * slots, 1), jnp.float32),
+            pltpu.VMEM((group * count, w_gate.shape[1]), jnp.bfloat16),
+        ],
+        compiler_params=pltpu.CompilerParams(vmem_limit_bytes=60 << 20),
+    )(every, weight, w_gate, w_up, w_down, s_gate, s_up, s_down)
+
+
+def reduce_kernel(wide, part, out, twin_in, diag_in, side_in, line_in, send, recv, local, acc):
+    me = lax.axis_index("wide")
+    core = lax.axis_index("narrow")
+    lines = wide // PLANE
+    count = out.shape[0]
+    half = count // 2
+    x_peer, y_peer, twin = (me ^ 1, core), (me ^ 2, core), (me, 1 - core)
+    zs = [(me ^ (PLANE * d), core) for d in range(1, lines)]
+    greet([twin, x_peer, y_peer] + zs)
+    T, XD, YD, X, Y, Z = 0, wide, wide + lines, wide + 2 * lines, wide + 3 * lines, wide + 4 * lines
+    started = []
+
+    def copy(number, source, target, device):
+        return pltpu.make_async_remote_copy(
+            src_ref=source,
+            dst_ref=target,
+            send_sem=send.at[number],
+            recv_sem=recv.at[number],
+            device_id=device,
+            device_id_type=MESH,
+        )
+
+    def start(item):
+        item.start()
+        started.append(item)
+
+    def arrive(number, place):
+        copy(number, place, place, twin).wait_recv()
+
+    step = 16
+
+    def add(target, sources, first, total):
+        def one(i, carry):
+            at = pl.ds(pl.multiple_of(first + i * step, step), step)
+            value = target[at].astype(jnp.float32)
+            for source, shift in sources:
+                value += source[pl.ds(pl.multiple_of(first + i * step - shift, step), step)].astype(
+                    jnp.float32
+                )
+            target[at] = value.astype(jnp.bfloat16)
+            return carry
+
+        lax.fori_loop(0, total // step, one, 0)
+
+    order = list(range(1, lines)) + [0]
+    chips = [flip ^ (PLANE * d) for flip in (3, 2, 1, 0) for d in order]
+    mine = []
+    for k in chips:
+        chip = me ^ k
+        start(copy(T + k, part.at[1 - core, chip], twin_in.at[k], twin))
+        item = pltpu.make_async_copy(part.at[core, chip], acc.at[k], local.at[k])
+        item.start()
+        mine.append(item)
+
+    def fold(k):
+        mine[chips.index(k)].wait()
+        arrive(T + k, twin_in.at[k])
+        add(acc.at[k], [(twin_in.at[k], 0)], 0, count)
+
+    for d in order:
+        k = 3 ^ (PLANE * d)
+        fold(k)
+        start(copy(XD + d, acc.at[k, pl.ds(0, half)], diag_in.at[0, d], x_peer))
+        start(copy(YD + d, acc.at[k, pl.ds(half, half)], diag_in.at[1, d], y_peer))
+    for d in order:
+        fold(2 ^ (PLANE * d))
+        fold(1 ^ (PLANE * d))
+    for d in order:
+        k = 2 ^ (PLANE * d)
+        arrive(XD + d, diag_in.at[0, d])
+        add(acc.at[k], [(diag_in.at[0, d], 0)], 0, half)
+        start(copy(Y + d, acc.at[k], side_in.at[1, d], y_peer))
+        k = 1 ^ (PLANE * d)
+        arrive(YD + d, diag_in.at[1, d])
+        add(acc.at[k], [(diag_in.at[1, d], half)], half, half)
+        start(copy(X + d, acc.at[k], side_in.at[0, d], x_peer))
+    for d in order:
+        fold(PLANE * d)
+    for d in order:
+        k = PLANE * d
+        arrive(X + d, side_in.at[0, d])
+        arrive(Y + d, side_in.at[1, d])
+        if d > 0:
+            add(acc.at[k], [(side_in.at[0, d], 0), (side_in.at[1, d], 0)], 0, count)
+            start(copy(Z + d, acc.at[k], line_in.at[d], (me ^ k, core)))
+    for d in range(1, lines):
+        arrive(Z + d, line_in.at[d])
+
+    def last(i, carry):
+        at = pl.ds(pl.multiple_of(i * step, step), step)
+        value = acc[0, at].astype(jnp.float32)
+        value += side_in[0, 0, at].astype(jnp.float32) + side_in[1, 0, at].astype(jnp.float32)
+        for d in range(1, lines):
+            value += line_in[d, at].astype(jnp.float32)
+        out[at] = value.astype(jnp.bfloat16)
+        return carry
+
+    lax.fori_loop(0, count // step, last, 0)
+    for item in started:
+        item.wait_send()
+
+
+def reduce(part):
+    narrow, wide, count, width = part.shape
+    lines = wide // PLANE
+    sems = wide + 5 * lines
+    bf16 = jnp.bfloat16
+    return pl.pallas_call(
+        functools.partial(reduce_kernel, wide),
+        out_shape=jax.ShapeDtypeStruct((count, width), bf16),
+        in_specs=[VMEM],
+        out_specs=VMEM,
+        scratch_shapes=[
+            pltpu.VMEM((wide, count, width), bf16),
+            pltpu.VMEM((2, lines, count // 2, width), bf16),
+            pltpu.VMEM((2, lines, count, width), bf16),
+            pltpu.VMEM((lines, count, width), bf16),
+            pltpu.SemaphoreType.DMA((sems,)),
+            pltpu.SemaphoreType.DMA((sems,)),
+            pltpu.SemaphoreType.DMA((wide,)),
+            pltpu.VMEM((wide, count, width), bf16),
+        ],
+        compiler_params=pltpu.CompilerParams(
+            collective_id=1, has_side_effects=True, vmem_limit_bytes=60 << 20
+        ),
+    )(part)
+
+
+def gather_body(
+    tokens,
+    expert_ids,
+    gate_weights,
+    shared_gate,
+    shared_up,
+    shared_down,
+    expert_gate,
+    expert_up,
+    expert_down,
+):
+    tok_count, top_count = expert_ids.shape
+    wide = lax.axis_size("wide")
+    narrow = lax.axis_size("narrow")
+    experts = wide * expert_gate.shape[0]
+    capacity, _ = plan(tok_count, top_count, experts, wide)
+    names = jnp.arange(experts, dtype=jnp.int32)
+    match = expert_ids.T[None, :, :] == names[:, None, None]
+    dense = jnp.sum(jnp.where(match, gate_weights.T[None, :, :], 0.0), axis=1)
+    dense = jnp.broadcast_to(dense[:, None, :], (experts, 8, tok_count))
+    every, s_gate, s_up, s_down, weight = gather(
+        wide, tokens, shared_gate, shared_up, shared_down, dense
+    )
+    part = expert(
+        capacity,
+        every,
+        weight,
+        expert_gate[0],
+        expert_up[0],
+        expert_down[0],
+        s_gate,
+        s_up,
+        s_down,
+        narrow,
+    )
+    return reduce(part)
+
+
 def solution(mesh):
     in_specs = (
         P("wide", None),
@@ -96,4 +539,11 @@
         P("wide", "narrow", None),
     )
     out_specs = P("wide", "narrow")
+    wide_count = mesh.shape["wide"]
+
+    def body(*args):
+        tok_count, top_count = args[1].shape
+        gathers = plan(tok_count, top_count, wide_count * args[6].shape[0], wide_count)[1]
+        return (gather_body if gathers else dispatch_body)(*args)
+
     return jax.shard_map(body, mesh=mesh, in_specs=in_specs, out_specs=out_specs, check_vma=False)

time: 463 us -> 170 us (0.37)
  waiting for transfers between devices: 321 us -> 0 us
  Pallas kernels: 0 us -> 159 us
  blocking collectives: 53.3 us -> 0 us
  matrix products: 31.1 us -> 0 us
  between operations: 14.9 us -> 0.02 us
  local copies, waits for them, and re-layouts: 21.7 us -> 9.73 us
  other arithmetic: 10.1 us -> 0.87 us
  starting transfers between devices: 6.8 us -> 0 us
    all_gather x4 -> x0, waiting for transfers between devices: 308 us -> none  [the longest x1 109 us: body(): lax.all_gather(shared_down, 'wide', axis=1, tiled=True)]
    pallas_call x0 -> x3, Pallas kernels: none -> 159 us  [the longest x1 68.3 us: gather(): pl.pallas_call(functools.partial(gather_kernel, wide), out_shape=(jax.Sha...]
    all_to_all x1 -> x0, blocking collectives: 53.3 us -> none  [body(): lax.all_to_all(own_rows, 'wide', split_axis=0, concat_axis=0, tiled=True)]
    dot_general x4 -> x0, matrix products: 31.1 us -> none  [the longest x1 11.3 us: expert_ffn(): jnp.dot(hidden, w_down, preferred_element_type=jnp.float32)]
    gather x2 -> x0, local copies, waits for them, and re-layouts: 12.4 us -> none  [the longest x1 6.42 us: body(): pair_rows = returned_rows[target_slot].astype(jnp.float32)]
    reduce_scatter x2 -> x0, waiting for transfers between devices: 11.5 us -> none  [the longest x1 11.4 us: body(): lax.psum_scatter(partial_value, 'narrow', scatter_dimension=2, tiled=True)]
    unnamed x8 -> x5, local copies, waits for them, and re-layouts: 1.02 us -> 9.1 us
    all_to_all x1 -> x0, starting transfers between devices: 6.41 us -> none  [body(): lax.all_to_all(expert_out, 'wide', split_axis=0, concat_axis=0, tiled=True)]
  transfers between devices with their start and end apart: 7 -> 0, of which waited for: 5 -> 0; matrix products, arithmetic and copies ran while one was open for 6% -> 0% of each run, Pallas kernels for 0% -> 0%
where the time goes in v1:
time: 170 us; the launch traced here: 169 us
  Pallas kernels  159 us (94%)
  local copies, waits for them, and re-layouts  9.73 us (6%)
    pallas_call x1, Pallas kernels, gather(): pl.pallas_call(functools.partial(gather_kernel, wide), out_shape=(jax.Sha...  68.3 us
    pallas_call x1, Pallas kernels, reduce(): pl.pallas_call(functools.partial(reduce_kernel, wide), out_shape=jax.Shap...  59.8 us
    pallas_call x1, Pallas kernels, expert(): pl.pallas_call(functools.partial(expert_kernel, group, slots), grid=(wide...  30.9 us
    unnamed x5, local copies, waits for them, and re-layouts  9.1 us

profile of v1, /device:TPU:17, one launch (start us, length us, event | category | flops | bytes accessed | tf_op | source)
XLA Modules:
  0.0 169.5 jit_solution(14662891067338692890)
XLA Ops:
  0.0 0.0 copy-start
  0.0 0.9 select_reduce_fusion
  0.9 0.6 broadcast_in_dim.23.dense
  1.5 4.6 %copy.12 = bf16[1,2048,704]{2,1,0:T(8,128)(2,1)} copy(bf16[1,2048,704]{1,2,0:T(8,128)(2,1)} %param.15) | data formatting | bytes 5767168 | tf_op args[6]
  6.1 0.0 copy-done
  6.1 2.8 %copy.13 = bf16[1,2048,704]{2,1,0:T(8,128)(2,1)} copy(bf16[1,2048,704]{1,2,0:T(8,128)(2,1)S(1)} %copy-done) | data formatting | bytes 5767168 | tf_op args[7]
  8.9 68.3 %shard_map.91 = (bf16[2048,2048]{1,0:T(8,128)(2,1)}, bf16[2048,128]{1,0:T(8,128)(2,1)}, bf16[2048,128]{1,0:T(8,128)(2,1)}, bf16[128,2048]{1,0:T(8,128)(2,1)}, f32[16,8,128]{2,1,0:T(8,128)}) custom-call(bf16[128,2048]{1,0:T(8,128)(2,1)} %tok.1, bf16[128,1408]{1,0:T(8,128)(2,1)} %gate.1, bf16[128,1408]{1,0:T(8,128)(2,1)} %up.1, bf16[1408,128]{1,0:T(8,128)(2,1)} %down.1, ...), custom_call_target="tpu_custom_call" | custom-call | tf_op jit(solution)/shard_map/pallas_call | solution.py:270
  77.2 30.9 %shard_map.92.part = bf16[2,16,128,1024]{3,2,1,0:T(8,128)(2,1)} custom-call(bf16[2048,2048]{1,0:T(8,128)(2,1)} %get-tuple-element.10.x, f32[16,8,128]{2,1,0:T(8,128)} %get-tuple-element.11.w, bf16[2048,704]{1,0:T(8,128)(2,1)} %bitcast.5, bf16[2048,704]{1,0:T(8,128)(2,1)} %bitcast.6, bf16[704,2048]{1,0:T(8,128)(2,1)} %bitcast.7, ...), custom_call_target="tpu_custom_call" | custom-call | tf_op jit(solution)/shard_map/pallas_call | solution.py:339
  108.0 59.8 %shard_map.93 = bf16[128,1024]{1,0:T(8,128)(2,1)} custom-call(bf16[2,16,128,1024]{3,2,1,0:T(8,128)(2,1)} %shard_map.92.part), custom_call_target="tpu_custom_call" | custom-call | tf_op jit(solution)/shard_map/pallas_call | solution.py:470
  167.8 1.7 copy.15
Async XLA Ops:
  0.0 6.1 %copy-start = (bf16[1,2048,704]{1,2,0:T(8,128)(2,1)S(1)}, bf16[1,2048,704]{1,2,0:T(8,128)(2,1)}, u32[]{:S(2)}) copy-start(bf16[1,2048,704]{1,2,0:T(8,128)(2,1)} %param.16) | copy-start | bytes 8650756

commit v2 on v0

--- a/solution.py
+++ b/solution.py
@@ -1,6 +1,10 @@
+import functools
+
 import jax
 import jax.numpy as jnp
 from jax import lax
+from jax.experimental import pallas as pl
+from jax.experimental.pallas import tpu as pltpu
 from jax.sharding import PartitionSpec as P
 
 
@@ -14,7 +18,7 @@
     return partial_value.reshape(senders, items, w_down.shape[1])
 
 
-def body(
+def dispatch_body(
     tokens,
     expert_ids,
     gate_weights,
@@ -83,6 +87,419 @@
     return (shared + routed).astype(jnp.bfloat16)
 
 
+MESH = pl.DeviceIdType.MESH
+ANY = pl.BlockSpec(memory_space=pl.ANY)
+VMEM = pl.BlockSpec(memory_space=pltpu.VMEM)
+LANES = 128
+PLANE = 4
+
+
+def plan(tok_count, top_count, experts, wide_count):
+    capacity = min(tok_count, 4 * tok_count * top_count // (3 * experts))
+    return capacity, wide_count * tok_count <= 4 * experts * capacity
+
+
+def greet(devices):
+    barrier = pltpu.get_barrier_semaphore()
+    for device in devices:
+        pl.semaphore_signal(barrier, inc=1, device_id=device, device_id_type=MESH)
+    pl.semaphore_wait(barrier, len(devices))
+
+
+def fused_kernel(
+    wide,
+    slots,
+    tok,
+    gate,
+    up,
+    down,
+    dense,
+    w_gate_in,
+    w_up_in,
+    w_down_in,
+    out,
+    every,
+    all_gate,
+    all_up,
+    all_down,
+    weight,
+    w_gate,
+    w_up,
+    w_down,
+    rows,
+    slot_w,
+    both,
+    other,
+    acc,
+    twin_in,
+    diag_in,
+    side_in,
+    line_in,
+    send,
+    recv,
+    local,
+):
+    f32, bf16 = jnp.float32, jnp.bfloat16
+    me = lax.axis_index("wide")
+    core = lax.axis_index("narrow")
+    lines = wide // PLANE
+    count = tok.shape[0]
+    share = count // 2
+    half = share // 2
+    pieces = gate.shape[1] // LANES
+    greet([(me ^ k, core) for k in range(1, wide)] + [(me, 1 - core)])
+    x_peer, y_peer, twin = (me ^ 1, core), (me ^ 2, core), (me, 1 - core)
+    started = []
+
+    def pos(k):
+        return (k % PLANE) * lines + k // PLANE
+
+    def copy(number, source, target, device):
+        return pltpu.make_async_remote_copy(
+            src_ref=source,
+            dst_ref=target,
+            send_sem=send.at[number],
+            recv_sem=recv.at[number],
+            device_id=device,
+            device_id_type=MESH,
+        )
+
+    def start(item):
+        item.start()
+        started.append(item)
+
+    def landed(number, place):
+        copy(number, place, place, twin).wait_recv()
+
+    def region(k, side=None, of=core):
+        begin = pos(k) * count + of * share
+        if side is None:
+            return every.at[pl.ds(pl.multiple_of(begin, share), share)]
+        return every.at[pl.ds(pl.multiple_of(begin + side * half, half), half)]
+
+    Z, X, Y, XD, YD, T = (lines * i for i in range(6))
+    W = T + 5 * lines
+    R = W + 4 * wide
+
+    def arrive(number, place):
+        landed(number, place)
+        start(copy(T + number, place, place, twin))
+
+    own = pltpu.make_async_copy(tok, every.at[pl.ds(0, count)], local.at[0])
+    own.start()
+    mine = tok.at[pl.ds(pl.multiple_of(core * share, share), share)]
+    start(copy(X, mine, region(1), x_peer))
+    start(copy(Y, mine, region(2), y_peer))
+    for d in range(1, lines):
+        start(copy(Z + d, mine, region(PLANE * d), (me ^ (PLANE * d), core)))
+    for k in range(1, wide):
+        start(copy(W + k, dense.at[me ^ k], weight.at[pos(k)], (me ^ k, core)))
+    loads = [pltpu.make_async_copy(dense.at[me], weight.at[0], local.at[1])]
+    for number, (source, target) in enumerate(
+        ((w_gate_in, w_gate), (w_up_in, w_up), (w_down_in, w_down))
+    ):
+        loads.append(pltpu.make_async_copy(source, target, local.at[5 + number]))
+    for item in loads:
+        item.start()
+
+    def shared_copies(k):
+        part = pl.ds(pl.multiple_of((me ^ k) * LANES, LANES), LANES)
+        place = pl.ds(pl.multiple_of(me * LANES, LANES), LANES)
+        to = (me ^ k, core)
+        return [
+            copy(W + k + wide, gate.at[:, part], all_gate.at[place], to),
+            copy(W + k + 2 * wide, up.at[:, part], all_up.at[place], to),
+            copy(W + k + 3 * wide, down.at[part], all_down.at[:, place], to),
+        ]
+
+    def send_shared(ks):
+        for k in ks:
+
+            @pl.when((me ^ k) < pieces)
+            def _():
+                for item in shared_copies(k):
+                    item.start()
+
+    def line(d):
+        arrive(Z + d, region(PLANE * d))
+        start(copy(X + d, region(PLANE * d), region(PLANE * d ^ 1), x_peer))
+        start(copy(Y + d, region(PLANE * d), region(PLANE * d ^ 2), y_peer))
+
+    def beside(d):
+        k = 1 ^ (PLANE * d)
+        arrive(X + d, region(k))
+        start(copy(YD + d, region(k, 1), region(k ^ 2, 1), y_peer))
+        k = 2 ^ (PLANE * d)
+        arrive(Y + d, region(k))
+        start(copy(XD + d, region(k, 0), region(k ^ 1, 0), x_peer))
+
+    send_shared(range(1, wide))
+    beside(0)
+    for d in range(1, lines):
+        line(d)
+        if d >= 2:
+            beside(d - 1)
+
+    @pl.when(me < pieces)
+    def _():
+        part = pl.ds(pl.multiple_of(me * LANES, LANES), LANES)
+        items = [
+            pltpu.make_async_copy(gate.at[:, part], all_gate.at[part], local.at[2]),
+            pltpu.make_async_copy(up.at[:, part], all_up.at[part], local.at[3]),
+            pltpu.make_async_copy(down.at[part], all_down.at[:, part], local.at[4]),
+        ]
+        for item in items:
+            item.start()
+        for item in items:
+            item.wait()
+
+    @pl.when(me >= pieces)
+    def _():
+        all_gate[...] = jnp.zeros_like(all_gate)
+        all_up[...] = jnp.zeros_like(all_up)
+        all_down[...] = jnp.zeros_like(all_down)
+
+    beside(lines - 1)
+
+    block = lines * count
+    lane_r = lax.broadcasted_iota(jnp.int32, (count, count), 0)
+    lane_c = lax.broadcasted_iota(jnp.int32, (count, count), 1)
+    upper = (lane_r <= lane_c).astype(f32).astype(bf16)
+    slot = lax.broadcasted_iota(jnp.int32, (slots, count), 0).astype(f32)
+
+    def across(a, b):
+        return lax.dot_general(a, b, (((1,), (1,)), ((), ())), preferred_element_type=f32)
+
+    def routed_hidden(group):
+        picks = []
+        for b in range(lines):
+            value = weight[group * lines + b]
+            chosen = (value > 0.0).astype(f32)
+            rank = jnp.dot(chosen.astype(bf16), upper, preferred_element_type=f32)
+            where = jnp.where(chosen > 0.0, rank - 1.0, -1.0)[0:1]
+            pick = (jnp.broadcast_to(where, (slots, count)) == slot).astype(f32)
+            picks.append(pick)
+            place = pl.ds(b * slots, slots)
+            slot_w[place] = jnp.sum(pick * value[0:1], axis=1, keepdims=True)
+            at = pl.ds(pl.multiple_of(group * block + b * count, count), count)
+            rows[place] = jnp.dot(
+                pick.astype(bf16), every[at], preferred_element_type=f32
+            ).astype(bf16)
+        gate_part = across(rows[...], w_gate[...])
+        up_part = across(rows[...], w_up[...])
+        hidden = (jax.nn.silu(gate_part) * up_part * slot_w[...]).astype(bf16)
+        for b in range(lines):
+            spread = jnp.dot(
+                picks[b].T.astype(bf16),
+                hidden[b * slots : (b + 1) * slots],
+                preferred_element_type=f32,
+            )
+            at = pl.ds(pl.multiple_of(group * block + b * count, count), count)
+            both[at] = spread.astype(bf16)
+
+    width = out.shape[1]
+
+    def finish(group):
+        at = pl.ds(pl.multiple_of(group * block, block), block)
+        gate_part = jnp.dot(every[at], all_gate[...], preferred_element_type=f32)
+        up_part = jnp.dot(every[at], all_up[...], preferred_element_type=f32)
+        shared = (jax.nn.silu(gate_part) * up_part).astype(bf16)
+        for target, which in ((other, 1 - core), (acc, core)):
+            columns = pl.ds(pl.multiple_of(which * width, width), width)
+            part = jnp.dot(both[at], w_down[:, columns], preferred_element_type=f32)
+            part += jnp.dot(shared, all_down[:, columns], preferred_element_type=f32)
+            target[at] = part.astype(bf16)
+
+    for k in range(1, wide):
+        landed(W + k, weight.at[pos(k)])
+    for item in loads:
+        item.wait()
+    own.wait()
+    for d in range(lines):
+        if d > 0:
+            landed(T + Z + d, region(PLANE * d, None, 1 - core))
+        landed(T + X + d, region(PLANE * d ^ 1, None, 1 - core))
+        landed(T + Y + d, region(PLANE * d ^ 2, None, 1 - core))
+
+    def early(group, carry):
+        routed_hidden(group)
+        return carry
+
+    lax.fori_loop(0, 3, early, 0)
+    for d in range(lines):
+        arrive(XD + d, region(3 ^ (PLANE * d), 0))
+        arrive(YD + d, region(3 ^ (PLANE * d), 1))
+    for d in range(lines):
+        landed(T + XD + d, region(3 ^ (PLANE * d), 0, 1 - core))
+        landed(T + YD + d, region(3 ^ (PLANE * d), 1, 1 - core))
+    routed_hidden(3)
+    for k in range(1, wide):
+
+        @pl.when(me < pieces)
+        def _():
+            place = pl.ds(pl.multiple_of((me ^ k) * LANES, LANES), LANES)
+            places = (all_gate.at[place], all_up.at[place], all_down.at[:, place])
+            for number, target in enumerate(places):
+                landed(W + k + (number + 1) * wide, target)
+
+    RT, RXD, RYD = R, R + wide, R + wide + lines
+    RX, RY, RZ = RYD + lines, RYD + 2 * lines, RYD + 3 * lines
+    step = 16
+
+    def rows_of(ref, k, begin=0, size=count):
+        return ref.at[pl.ds(pos(k) * count + begin, size)]
+
+    def add(target, sources):
+        def one(i, carry):
+            at = pl.ds(pl.multiple_of(i * step, step), step)
+            value = target[at].astype(f32)
+            for source in sources:
+                value += source[at].astype(f32)
+            target[at] = value.astype(bf16)
+            return carry
+
+        lax.fori_loop(0, target.shape[0] // step, one, 0)
+
+    def hand_over(flip):
+        finish(flip)
+        for d in range(lines):
+            k = flip ^ (PLANE * d)
+            start(copy(RT + k, rows_of(other, k), rows_of(twin_in, k), twin))
+
+    def fold(k):
+        landed(RT + k, rows_of(twin_in, k))
+        add(rows_of(acc, k), [rows_of(twin_in, k)])
+
+    order = list(range(1, lines)) + [0]
+    tall = count // 2
+    hand_over(3)
+    for d in order:
+        k = 3 ^ (PLANE * d)
+        fold(k)
+        start(copy(RXD + d, rows_of(acc, k, 0, tall), diag_in.at[0, d], x_peer))
+        start(copy(RYD + d, rows_of(acc, k, tall, tall), diag_in.at[1, d], y_peer))
+    hand_over(2)
+    hand_over(1)
+    for d in order:
+        k = 2 ^ (PLANE * d)
+        fold(k)
+        landed(RXD + d, diag_in.at[0, d])
+        add(rows_of(acc, k, 0, tall), [diag_in.at[0, d]])
+        start(copy(RY + d, rows_of(acc, k), side_in.at[1, d], y_peer))
+        k = 1 ^ (PLANE * d)
+        fold(k)
+        landed(RYD + d, diag_in.at[1, d])
+        add(rows_of(acc, k, tall, tall), [diag_in.at[1, d]])
+        start(copy(RX + d, rows_of(acc, k), side_in.at[0, d], x_peer))
+    hand_over(0)
+    for d in order:
+        fold(PLANE * d)
+    for d in order:
+        k = PLANE * d
+        landed(RX + d, side_in.at[0, d])
+        landed(RY + d, side_in.at[1, d])
+        if d > 0:
+            add(rows_of(acc, k), [side_in.at[0, d], side_in.at[1, d]])
+            start(copy(RZ + d, rows_of(acc, k), line_in.at[d], (me ^ k, core)))
+    for d in range(1, lines):
+        landed(RZ + d, line_in.at[d])
+
+    def last(i, carry):
+        at = pl.ds(pl.multiple_of(i * step, step), step)
+        value = acc[at].astype(f32)
+        value += side_in[0, 0, at].astype(f32) + side_in[1, 0, at].astype(f32)
+        for d in range(1, lines):
+            value += line_in[d, at].astype(f32)
+        out[at] = value.astype(bf16)
+        return carry
+
+    lax.fori_loop(0, count // step, last, 0)
+    for k in range(1, wide):
+
+        @pl.when((me ^ k) < pieces)
+        def _():
+            for item in shared_copies(k):
+                item.wait_send()
+
+    for item in started:
+        item.wait_send()
+
+
+def fused(wide, narrow, slots, tokens, gate, up, down, dense, w_gate, w_up, w_down):
+    count, width = tokens.shape
+    part = width // narrow
+    lines = wide // PLANE
+    total = wide * count
+    sems = 10 * lines + 4 * wide + wide + 5 * lines
+    bf16, f32 = jnp.bfloat16, jnp.float32
+    return pl.pallas_call(
+        functools.partial(fused_kernel, wide, slots),
+        out_shape=jax.ShapeDtypeStruct((count, part), bf16),
+        in_specs=[VMEM] * 5 + [ANY] * 3,
+        out_specs=VMEM,
+        scratch_shapes=[
+            pltpu.VMEM((total, width), bf16),
+            pltpu.VMEM((wide * gate.shape[0], LANES), bf16),
+            pltpu.VMEM((wide * gate.shape[0], LANES), bf16),
+            pltpu.VMEM((LANES, wide * down.shape[1]), bf16),
+            pltpu.VMEM((wide, 8, count), f32),
+            pltpu.VMEM(w_gate.shape, bf16),
+            pltpu.VMEM(w_up.shape, bf16),
+            pltpu.VMEM(w_down.shape, bf16),
+            pltpu.VMEM((lines * slots, width), bf16),
+            pltpu.VMEM((lines * slots, 1), f32),
+            pltpu.VMEM((total, w_gate.shape[0]), bf16),
+            pltpu.VMEM((total, part), bf16),
+            pltpu.VMEM((total, part), bf16),
+            pltpu.VMEM((total, part), bf16),
+            pltpu.VMEM((2, lines, count // 2, part), bf16),
+            pltpu.VMEM((2, lines, count, part), bf16),
+            pltpu.VMEM((lines, count, part), bf16),
+            pltpu.SemaphoreType.DMA((sems,)),
+            pltpu.SemaphoreType.DMA((sems,)),
+            pltpu.SemaphoreType.DMA((8,)),
+        ],
+        compiler_params=pltpu.CompilerParams(
+            collective_id=0, has_side_effects=True, vmem_limit_bytes=63 << 20
+        ),
+    )(tokens, gate, up, down, dense, w_gate, w_up, w_down)
+
+
+def gather_body(
+    tokens,
+    expert_ids,
+    gate_weights,
+    shared_gate,
+    shared_up,
+    shared_down,
+    expert_gate,
+    expert_up,
+    expert_down,
+):
+    tok_count, top_count = expert_ids.shape
+    wide = lax.axis_size("wide")
+    narrow = lax.axis_size("narrow")
+    experts = wide * expert_gate.shape[0]
+    capacity, _ = plan(tok_count, top_count, experts, wide)
+    names = jnp.arange(experts, dtype=jnp.int32)
+    match = expert_ids.T[None, :, :] == names[:, None, None]
+    dense = jnp.sum(jnp.where(match, gate_weights.T[None, :, :], 0.0), axis=1)
+    dense = jnp.broadcast_to(dense[:, None, :], (experts, 8, tok_count))
+    return fused(
+        wide,
+        narrow,
+        capacity,
+        tokens,
+        shared_gate,
+        shared_up,
+        shared_down,
+        dense,
+        expert_gate[0].T,
+        expert_up[0].T,
+        expert_down[0],
+    )
+
+
 def solution(mesh):
     in_specs = (
         P("wide", None),
@@ -96,4 +513,11 @@
         P("wide", "narrow", None),
     )
     out_specs = P("wide", "narrow")
+    wide_count = mesh.shape["wide"]
+
+    def body(*args):
+        tok_count, top_count = args[1].shape
+        gathers = plan(tok_count, top_count, wide_count * args[6].shape[0], wide_count)[1]
+        return (gather_body if gathers else dispatch_body)(*args)
+
     return jax.shard_map(body, mesh=mesh, in_specs=in_specs, out_specs=out_specs, check_vma=False)

time: 463 us -> 126 us (0.27)
  waiting for transfers between devices: 321 us -> 0 us
  Pallas kernels: 0 us -> 123 us
  blocking collectives: 53.3 us -> 0 us
  matrix products: 31.1 us -> 0 us
  local copies, waits for them, and re-layouts: 21.7 us -> 2.3 us
  between operations: 14.9 us -> 0.01 us
  other arithmetic: 10.1 us -> 0.72 us
  starting transfers between devices: 6.8 us -> 0 us
    all_gather x4 -> x0, waiting for transfers between devices: 308 us -> none  [the longest x1 109 us: body(): lax.all_gather(shared_down, 'wide', axis=1, tiled=True)]
    pallas_call x0 -> x1, Pallas kernels: none -> 123 us  [fused(): pl.pallas_call(functools.partial(fused_kernel, wide, slots), out_shape=ja...]
    all_to_all x1 -> x0, blocking collectives: 53.3 us -> none  [body(): lax.all_to_all(own_rows, 'wide', split_axis=0, concat_axis=0, tiled=True)]
    dot_general x4 -> x0, matrix products: 31.1 us -> none  [the longest x1 11.3 us: expert_ffn(): jnp.dot(hidden, w_down, preferred_element_type=jnp.float32)]
    gather x2 -> x0, local copies, waits for them, and re-layouts: 12.4 us -> none  [the longest x1 6.42 us: body(): pair_rows = returned_rows[target_slot].astype(jnp.float32)]
    reduce_scatter x2 -> x0, waiting for transfers between devices: 11.5 us -> none  [the longest x1 11.4 us: body(): lax.psum_scatter(partial_value, 'narrow', scatter_dimension=2, tiled=True)]
    all_to_all x1 -> x0, starting transfers between devices: 6.41 us -> none  [body(): lax.all_to_all(expert_out, 'wide', split_axis=0, concat_axis=0, tiled=True)]
  transfers between devices with their start and end apart: 7 -> 0, of which waited for: 5 -> 0; matrix products, arithmetic and copies ran while one was open for 6% -> 0% of each run, Pallas kernels for 0% -> 0%
where the time goes in v2:
time: 126 us
  Pallas kernels  123 us (98%)
  local copies, waits for them, and re-layouts  2.3 us (2%)
    pallas_call x1, Pallas kernels, fused(): pl.pallas_call(functools.partial(fused_kernel, wide, slots), out_shape=ja...  123 us

profile of v2, /device:TPU:17, one launch (start us, length us, event | category | flops | bytes accessed | tf_op | source)
XLA Modules:
  0.0 125.7 jit_solution(7111670113597535038)
XLA Ops:
  0.0 0.7 select_reduce_fusion
  0.7 0.6 broadcast_in_dim.23.dense
  1.4 122.7 %shard_map.91 = bf16[128,1024]{1,0:T(8,128)(2,1)} custom-call(bf16[128,2048]{1,0:T(8,128)(2,1)} %tok.1, bf16[128,1408]{1,0:T(8,128)(2,1)} %gate.1, bf16[128,1408]{1,0:T(8,128)(2,1)} %up.1, bf16[1408,128]{1,0:T(8,128)(2,1)} %down.1, f32[16,8,128]{2,1,0:T(8,128)} %broadcast_in_dim.23.dense, bf16[704,2048]{1,0:T(8,128)(2,1)} %bitcast.9, ...), custom_call_target="tpu_custom_call" | custom-call | tf_op jit(solution)/shard_map/pallas_call | solution.py:435
  124.1 1.7 %copy.11 = bf16[128,1024]{1,0:T(8,128)(2,1)} copy(bf16[128,1024]{1,0:T(8,128)(2,1)} %shard_map.91) | data formatting | bytes 524288

commit v3 on v2

--- a/solution.py
+++ b/solution.py
@@ -259,8 +259,6 @@
         all_up[...] = jnp.zeros_like(all_up)
         all_down[...] = jnp.zeros_like(all_down)
 
-    beside(lines - 1)
-
     block = lines * count
     lane_r = lax.broadcasted_iota(jnp.int32, (count, count), 0)
     lane_c = lax.broadcasted_iota(jnp.int32, (count, count), 1)
@@ -315,9 +313,11 @@
     for item in loads:
         item.wait()
     own.wait()
+    for d in range(1, lines):
+        landed(T + Z + d, region(PLANE * d, None, 1 - core))
+    routed_hidden(0)
+    beside(lines - 1)
     for d in range(lines):
-        if d > 0:
-            landed(T + Z + d, region(PLANE * d, None, 1 - core))
         landed(T + X + d, region(PLANE * d ^ 1, None, 1 - core))
         landed(T + Y + d, region(PLANE * d ^ 2, None, 1 - core))
 
@@ -325,7 +325,7 @@
         routed_hidden(group)
         return carry
 
-    lax.fori_loop(0, 3, early, 0)
+    lax.fori_loop(1, 3, early, 0)
     for d in range(lines):
         arrive(XD + d, region(3 ^ (PLANE * d), 0))
         arrive(YD + d, region(3 ^ (PLANE * d), 1))
@@ -370,7 +370,7 @@
         landed(RT + k, rows_of(twin_in, k))
         add(rows_of(acc, k), [rows_of(twin_in, k)])
 
-    order = list(range(1, lines)) + [0]
+    order = list(range(lines - 1, 0, -1)) + [0]
     tall = count // 2
     hand_over(3)
     for d in order:

time: 126 us -> 121 us (0.960)
  the two profiles are of different devices: /device:TPU:17 before, /device:TPU:24 now
where the time goes in v3:
time: 121 us
  Pallas kernels  118 us (98%)
  local copies, waits for them, and re-layouts  2.3 us (2%)
    pallas_call x1, Pallas kernels, fused(): pl.pallas_call(functools.partial(fused_kernel, wide, slots), out_shape=ja...  118 us

profile of v3, /device:TPU:24, one launch (start us, length us, event | category | flops | bytes accessed | tf_op | source)
XLA Modules:
  0.0 120.8 jit_solution(8871451005376386091)
XLA Ops:
  0.0 0.7 select_reduce_fusion
  0.7 0.6 broadcast_in_dim.23.dense
  1.4 117.8 %shard_map.91 = bf16[128,1024]{1,0:T(8,128)(2,1)} custom-call(bf16[128,2048]{1,0:T(8,128)(2,1)} %tok.1, bf16[128,1408]{1,0:T(8,128)(2,1)} %gate.1, bf16[128,1408]{1,0:T(8,128)(2,1)} %up.1, bf16[1408,128]{1,0:T(8,128)(2,1)} %down.1, f32[16,8,128]{2,1,0:T(8,128)} %broadcast_in_dim.23.dense, bf16[704,2048]{1,0:T(8,128)(2,1)} %bitcast.9, ...), custom_call_target="tpu_custom_call" | custom-call | tf_op jit(solution)/shard_map/pallas_call | solution.py:435
  119.2 1.7 %copy.11 = bf16[128,1024]{1,0:T(8,128)(2,1)} copy(bf16[128,1024]{1,0:T(8,128)(2,1)} %shard_map.91) | data formatting | bytes 524288
